TPU v7x, 256 devices: a whole 4x4x8 slice. The times are simulated.
256 devices in a mesh: row: 16 (over x_hi, z), col: 8 (over x_lo, y), rep: 2 (over core).
Axes of the slice: x: 4 (x_hi: 2, x_lo: 2; x = x_hi * 2 + x_lo), y: 4, z: 8, core: 2. Of those that a mesh axis runs over, the one named last changes fastest.
Arguments:
- matrix: float32 [16384, 16384], P('row', 'col'), may hold values from -0.125 to 0.125
- vectors: float32 [64, 16384], P('rep', 'row'), may hold values from -0.3 to 0.3
Outputs:
- result: float32 [64, 16384], P('rep', 'row')
All inputs are finite; a program needn't handle non-finite values.
Results may differ from a plain program's by a relative error of at most 0.00011.
Values sent between devices are 32-bit elements; how exact they have to be, the bound alone decides.
No kernel may reach another device: no remote copies, remote signals or barrier semaphores. Data moves between devices by JAX's collectives and lax.ppermute only.
A program may use at most 64 MiB of HBM per device.

v0:
```python
import functools

import jax
import jax.numpy as jnp
from jax import lax
from jax.experimental import pallas as pl
from jax.experimental.pallas import tpu as pltpu
from jax.sharding import Mesh, PartitionSpec as P

TERMS = 6
STEPS = 1

ROW = ("xh", "zh", "zl")
COL = ("xl", "y")
SIZES = {"xh": 2, "zh": 4, "zl": 2, "xl": 2, "y": 4, "rep": 2}
PLACES = [
    (xh, zh, zl, xl, y)
    for xh in range(2)
    for zh in range(4)
    for zl in range(2)
    for xl in range(2)
    for y in range(4)
]
FAR = 2
ARRIVALS = (3, 1, 2)


def index(xh, zh, zl, xl, y):
    return (((xh * 4 + zh) * 2 + zl) * 2 + xl) * 4 + y


def owner_moves():
    def across(zh, y):
        return y if (y - zh) % 2 else (y + FAR) % 4

    return [
        (index(xh, zh, zl, xl, y), index(xl, across(zh, y), zl ^ int(y == zh), xh, zh))
        for xh, zh, zl, xl, y in PLACES
    ]


def partner_moves(which):
    return [
        (index(xh, zh, zl, xl, y), index(xh, zh ^ (which // 2), zl ^ (which % 2), xl, y))
        for xh, zh, zl, xl, y in PLACES
    ]


def held_half(zh):
    swapped = lax.rem(lax.axis_index("y") + FAR, 4) == zh
    return lax.axis_index("zl") ^ swapped.astype(jnp.int32)


def split(value):
    high = value.astype(jnp.bfloat16)
    low = (value - high.astype(jnp.float32)).astype(jnp.bfloat16)
    return high, low


def prepare_kernel(a_ref, high_ref, low_ref, held, sems):
    blocks = held.shape[0]
    width = held.shape[2]
    zh = lax.axis_index("zh")
    own_half, pair_half = held_half(zh), held_half(zh ^ 1)
    own_side = zh & 1

    def copy(block):
        column = pl.multiple_of(block * width, width)
        return pltpu.make_async_copy(a_ref.at[:, pl.ds(column, width)], held.at[block], sems.at[block])

    for block in range(blocks):
        copy(block).start()

    def step(block, carry):
        copy(block).wait()
        high, low = split(held[block].T)
        half, side, part = block // 4, lax.rem(block // 2, 2), lax.rem(block, 2)
        away = side ^ own_side
        first = own_half + away * (pair_half - own_half)
        place = ((half ^ first) + 2 * away) * 2 + part
        rows = pl.ds(pl.multiple_of(place * width, width), width)
        high_ref[rows, :] = high
        low_ref[rows, :] = low
        return carry

    lax.fori_loop(0, blocks, step, 0)


def prepare(matrix):
    rows, columns = matrix.shape
    width = columns // 8
    half = pltpu.VMEM((columns, rows), jnp.bfloat16)
    return pl.pallas_call(
        prepare_kernel,
        out_shape=(half, half),
        in_specs=[pl.BlockSpec(memory_space=pltpu.HBM)],
        out_specs=(pl.BlockSpec(memory_space=pltpu.VMEM),) * 2,
        scratch_shapes=[
            pltpu.VMEM((8, rows, width), jnp.float32),
            pltpu.SemaphoreType.DMA((8,)),
        ],
        cost_estimate=pl.CostEstimate(flops=4_000_000_000, bytes_accessed=8 << 20, transcendentals=0),
        compiler_params=pltpu.CompilerParams(vmem_limit_bytes=24 << 20),
    )(pltpu.with_memory_space_constraint(matrix, pltpu.HBM))


def tiles(pieces, high_ref, low_ref, before_ref=None):
    depth = high_ref.shape[0] // 4
    operands = []
    for quarter, piece in pieces:
        x_high, x_low = split(piece)
        rows = pl.ds(pl.multiple_of(quarter * depth, depth), depth)
        operands.append((rows, x_high, jnp.concatenate([x_high, x_low], axis=0)))
    for start in range(0, high_ref.shape[1], 256):
        columns = slice(start, start + 256)
        total = None
        for rows, x_high, both in operands:
            vectors = x_high.shape[0]
            first = jnp.dot(both, high_ref[rows, columns], preferred_element_type=jnp.float32)
            second = jnp.dot(x_high, low_ref[rows, columns], preferred_element_type=jnp.float32)
            value = first[:vectors] + (first[vectors:] + second)
            total = value if total is None else total + value
        if before_ref is not None:
            total = before_ref[:, columns] + total
        yield start, total


def block_pieces(which, x_ref):
    width = x_ref.shape[1] // 2
    zh = lax.axis_index("zh")
    side = zh & 1
    differs = held_half(zh) ^ held_half(zh ^ 1)
    at = [pl.multiple_of(place * width, width) for place in (side, 1 - side)]
    quarters = (which, 2 + (differs ^ which))
    return [(quarter, x_ref[:, pl.ds(place, width)]) for quarter, place in zip(quarters, at)]


def store(start, total, out_ref):
    out_ref[:, start : start + 256] = total


def spread(start, total, out_ref):
    side, within = divmod(start, out_ref.shape[2])
    for copy in range(4):
        out_ref[copy * 2 + side, :, within : within + 256] = total


def own_block_kernel(x_ref, high_ref, low_ref, vectors_ref, out_ref, running_ref):
    width = running_ref.shape[1]
    running_ref[...] = vectors_ref[:, pl.ds(pl.multiple_of((lax.axis_index("y") & 1) * width, width), width)]
    for start, total in tiles(block_pieces(0, x_ref), high_ref, low_ref):
        store(start, total, out_ref)


def other_block_kernel(x_ref, high_ref, low_ref, before_ref, out_ref):
    for start, total in tiles(block_pieces(1, x_ref), high_ref, low_ref, before_ref):
        spread(start, total, out_ref)


def own_kernel(x_ref, high_ref, low_ref, out_ref):
    for start, total in tiles([(0, x_ref[...])], high_ref, low_ref):
        store(start, total, out_ref)


def next_kernel(which, x_ref, high_ref, low_ref, before_ref, out_ref):
    for start, total in tiles([(which, x_ref[...])], high_ref, low_ref, before_ref):
        store(start, total, out_ref)


def spread_kernel(which, x_ref, high_ref, low_ref, before_ref, out_ref):
    for start, total in tiles([(which, x_ref[...])], high_ref, low_ref, before_ref):
        spread(start, total, out_ref)


def last_kernel(which, scale, x_ref, high_ref, low_ref, before_ref, running_ref, out_ref):
    width = running_ref.shape[1]
    mine = lax.axis_index("y")
    first = lax.axis_index("xl") == 0
    for start, total in tiles([(which, x_ref[...])], high_ref, low_ref, before_ref):
        side, within = divmod(start, width)
        running = running_ref[:, within : within + 256]
        adds = jnp.logical_and(first, mine == side)
        total = total / scale + jnp.where(adds, running, jnp.zeros_like(running))
        for copy in range(8):
            out_ref[copy, :, start : start + 256] = total


def combine_kernel(scale, parts_ref, running_ref, summand_ref, total_ref):
    summand = parts_ref[0]
    for part in range(1, parts_ref.shape[0]):
        summand = summand + parts_ref[part]
    summand = summand / scale
    summand_ref[...] = summand
    total_ref[...] = running_ref[...] + summand


def call(kernel, out, flops, limit, *operands):
    vmem = pl.BlockSpec(memory_space=pltpu.VMEM)
    shapes = jax.tree.map(lambda shape: jax.ShapeDtypeStruct(shape, jnp.float32), out, is_leaf=lambda o: isinstance(o[0], int))
    return pl.pallas_call(
        kernel,
        out_shape=shapes,
        in_specs=[vmem] * len(operands),
        out_specs=jax.tree.map(lambda _: vmem, shapes),
        cost_estimate=pl.CostEstimate(flops=flops, bytes_accessed=4 << 20, transcendentals=0),
        compiler_params=pltpu.CompilerParams(vmem_limit_bytes=limit),
    )(*operands)


def permute(value, moves):
    return lax.ppermute(value, ROW + COL, moves)


def exchange(value):
    return lax.all_to_all(value, COL, 0, 0, tiled=True)


FLOPS, LIMIT = 100_000_000, 4 << 20


def block_product(block, halves, vectors):
    count, width = block.shape
    other = permute(block, partner_moves(1))
    out = ((count, width), (count, width // 2))
    total, running = call(own_block_kernel, out, 2 * FLOPS, LIMIT, block, *halves, vectors)
    return call(other_block_kernel, (8, count, width // 2), 2 * FLOPS, LIMIT, other, *halves, total), running


def product(piece, halves, scale=None, running=None):
    vectors, width = piece.shape
    rows = halves[0].shape[1]
    others = {}
    for which in ARRIVALS:
        others[which] = permute(piece, partner_moves(which))
    total = call(own_kernel, (vectors, rows), FLOPS, LIMIT, piece, *halves)
    for which in ARRIVALS[:2]:
        kernel = functools.partial(next_kernel, which)
        total = call(kernel, (vectors, rows), FLOPS, LIMIT, others[which], *halves, total)
    which = ARRIVALS[2]
    if running is None:
        kernel = functools.partial(spread_kernel, which)
        return call(kernel, (8, vectors, width), FLOPS, LIMIT, others[which], *halves, total)
    kernel = functools.partial(last_kernel, which, scale)
    return call(kernel, (8, vectors, rows), FLOPS, LIMIT, others[which], *halves, total, running)


def local(matrix, vectors):
    block = permute(vectors, owner_moves())
    halves = prepare(matrix)
    block, halves = lax.optimization_barrier((block, halves))
    partial_value, running = block_product(block, halves, vectors)
    parts = exchange(partial_value)
    for degree in range(1, TERMS):
        kernel = functools.partial(combine_kernel, float(degree * STEPS))
        summand, running = call(kernel, (running.shape,) * 2, 1_000_000, 2 << 20, parts, running)
        piece = permute(summand, owner_moves())
        if degree + 1 < TERMS:
            parts = exchange(product(piece, halves))
        else:
            parts = exchange(product(piece, halves, float(TERMS * STEPS), running))
    return functools.reduce(jnp.add, [parts[part] for part in range(8)])


def solution(mesh):
    fine = Mesh(mesh.devices.reshape(tuple(SIZES.values())), tuple(SIZES))
    placed = (P(ROW, COL), P("rep", ROW))
    return jax.shard_map(local, mesh=fine, in_specs=placed, out_specs=P("rep", ROW), check_vma=False)
```

profile of v0, /device:TPU:2, one launch (start us, length us, event | category | flops | bytes accessed | tf_op | source)
XLA Modules:
  0.0 183.3 jit_solution(14403789643065036922)
XLA Ops:
  0.0 7.7 %collective-permute-start = (f32[32,1024]{1,0:T(8,128)}, f32[32,1024]{1,0:T(8,128)S(1)}, u32[]{:S(2)}, u32[]{:S(2)}) collective-permute-start(f32[32,1024]{1,0:T(8,128)} %vectors_ref.1), channel_id=1, source_target_pairs={{0,80},{2,32},{4,0},{6,96},{8,208},{10,160},{12,128},{14,224},{16,... | collective-permute-start | bytes 393224 | tf_op jit(solution)/shard_map/ppermute | solution.py:211
  7.7 4.3 %shard_map.28 = (bf16[2048,1024]{1,0:T(8,128)(2,1)S(1)}, bf16[2048,1024]{1,0:T(8,128)(2,1)S(1)}) custom-call(f32[1024,2048]{1,0:T(8,128)} %a_ref.1), custom_call_target="tpu_custom_call" | custom-call | flops 4000000000 | bytes 8388608 | tf_op jit(solution)/shard_map/pallas_call | solution.py:93
  13.9 3.1 %collective-permute-done.1.x_ref = f32[32,1024]{1,0:T(8,128)S(1)} collective-permute-done((f32[32,1024]{1,0:T(8,128)S(1)}, f32[32,1024]{1,0:T(8,128)S(1)}, u32[]{:S(2)}, u32[]{:S(2)}) %collective-permute-start.1) | collective-permute-done | bytes 131104 | tf_op jit(solution)/shard_map/ppermute | solution.py:211
  17.9 15.4 %all_to_all.30.parts_ref = f32[8,32,512]{2,1,0:T(8,128)S(1)} all-to-all(f32[8,32,512]{2,1,0:T(8,128)S(1)} %shard_map.30), channel_id=1, replica_groups=mesh['xh'=2,'zh'=4,'zl'=2,'xl'=2,'y'=4,'rep'=2] {'xl','y'}, dimensions={0} | all-to-all | bytes 1048576 | tf_op jit(solution)/shard_map/all_to_all | solution.py:215
  33.3 4.0 %collective-permute-start.2 = (f32[32,512]{1,0:T(8,128)S(1)}, f32[32,512]{1,0:T(8,128)S(1)}, u32[]{:S(2)}, u32[]{:S(2)}) collective-permute-start(f32[32,512]{1,0:T(8,128)S(1)} %get-tuple-element.29), channel_id=1, source_target_pairs={{0,80},{2,32},{4,0},{6,96},{8,208},{10,160},{12,128},{14,224},{16,... | collective-permute-start | bytes 196616 | tf_op jit(solution)/shard_map/ppermute | solution.py:211
  37.3 2.9 %collective-permute-done.2.x_ref = f32[32,512]{1,0:T(8,128)S(1)} collective-permute-done((f32[32,512]{1,0:T(8,128)S(1)}, f32[32,512]{1,0:T(8,128)S(1)}, u32[]{:S(2)}, u32[]{:S(2)}) %collective-permute-start.2) | collective-permute-done | bytes 65568 | tf_op jit(solution)/shard_map/ppermute | solution.py:211
  40.2 3.2 %collective-permute-start.5 = (f32[32,512]{1,0:T(8,128)S(1)}, f32[32,512]{1,0:T(8,128)S(1)}, u32[]{:S(2)}, u32[]{:S(2)}) collective-permute-start(f32[32,512]{1,0:T(8,128)S(1)} %collective-permute-done.2.x_ref), channel_id=1, source_target_pairs={{0,48},{2,50},{4,52},{6,54},{8,56},{10,58},{12,60},{14,62},{16,32}... | collective-permute-start | bytes 196616 | tf_op jit(solution)/shard_map/ppermute | solution.py:211
  49.1 12.8 %all_to_all.31.parts_ref = f32[8,32,512]{2,1,0:T(8,128)S(1)} all-to-all(f32[8,32,512]{2,1,0:T(8,128)S(1)} %shard_map.35), channel_id=1, replica_groups=mesh['xh'=2,'zh'=4,'zl'=2,'xl'=2,'y'=4,'rep'=2] {'xl','y'}, dimensions={0} | all-to-all | bytes 1048576 | tf_op jit(solution)/shard_map/all_to_all | solution.py:215
  61.8 5.5 %collective-permute-start.6 = (f32[32,512]{1,0:T(8,128)S(1)}, f32[32,512]{1,0:T(8,128)S(1)}, u32[]{:S(2)}, u32[]{:S(2)}) collective-permute-start(f32[32,512]{1,0:T(8,128)S(1)} %get-tuple-element.31), channel_id=1, source_target_pairs={{0,80},{2,32},{4,0},{6,96},{8,208},{10,160},{12,128},{14,224},{16,... | collective-permute-start | bytes 196616 | tf_op jit(solution)/shard_map/ppermute | solution.py:211
  67.3 1.9 %collective-permute-done.6.x_ref = f32[32,512]{1,0:T(8,128)S(1)} collective-permute-done((f32[32,512]{1,0:T(8,128)S(1)}, f32[32,512]{1,0:T(8,128)S(1)}, u32[]{:S(2)}, u32[]{:S(2)}) %collective-permute-start.6) | collective-permute-done | bytes 65568 | tf_op jit(solution)/shard_map/ppermute | solution.py:211
  69.3 5.0 %collective-permute-start.9 = (f32[32,512]{1,0:T(8,128)S(1)}, f32[32,512]{1,0:T(8,128)S(1)}, u32[]{:S(2)}, u32[]{:S(2)}) collective-permute-start(f32[32,512]{1,0:T(8,128)S(1)} %collective-permute-done.6.x_ref), channel_id=1, source_target_pairs={{0,48},{2,50},{4,52},{6,54},{8,56},{10,58},{12,60},{14,62},{16,32}... | collective-permute-start | bytes 196616 | tf_op jit(solution)/shard_map/ppermute | solution.py:211
  80.0 12.3 %all_to_all.32.parts_ref = f32[8,32,512]{2,1,0:T(8,128)S(1)} all-to-all(f32[8,32,512]{2,1,0:T(8,128)S(1)} %shard_map.40), channel_id=1, replica_groups=mesh['xh'=2,'zh'=4,'zl'=2,'xl'=2,'y'=4,'rep'=2] {'xl','y'}, dimensions={0} | all-to-all | bytes 1048576 | tf_op jit(solution)/shard_map/all_to_all | solution.py:215
  92.3 4.2 %collective-permute-start.10 = (f32[32,512]{1,0:T(8,128)S(1)}, f32[32,512]{1,0:T(8,128)S(1)}, u32[]{:S(2)}, u32[]{:S(2)}) collective-permute-start(f32[32,512]{1,0:T(8,128)S(1)} %get-tuple-element.33), channel_id=1, source_target_pairs={{0,80},{2,32},{4,0},{6,96},{8,208},{10,160},{12,128},{14,224},{16,... | collective-permute-start | bytes 196616 | tf_op jit(solution)/shard_map/ppermute | solution.py:211
  96.6 2.5 %collective-permute-done.10.x_ref = f32[32,512]{1,0:T(8,128)S(1)} collective-permute-done((f32[32,512]{1,0:T(8,128)S(1)}, f32[32,512]{1,0:T(8,128)S(1)}, u32[]{:S(2)}, u32[]{:S(2)}) %collective-permute-start.10) | collective-permute-done | bytes 65568 | tf_op jit(solution)/shard_map/ppermute | solution.py:211
  99.1 2.6 %collective-permute-start.13 = (f32[32,512]{1,0:T(8,128)S(1)}, f32[32,512]{1,0:T(8,128)S(1)}, u32[]{:S(2)}, u32[]{:S(2)}) collective-permute-start(f32[32,512]{1,0:T(8,128)S(1)} %collective-permute-done.10.x_ref), channel_id=1, source_target_pairs={{0,48},{2,50},{4,52},{6,54},{8,56},{10,58},{12,60},{14,62},{16,32}... | collective-permute-start | bytes 196616 | tf_op jit(solution)/shard_map/ppermute | solution.py:211
  107.3 13.7 %all_to_all.33.parts_ref = f32[8,32,512]{2,1,0:T(8,128)S(1)} all-to-all(f32[8,32,512]{2,1,0:T(8,128)S(1)} %shard_map.45), channel_id=1, replica_groups=mesh['xh'=2,'zh'=4,'zl'=2,'xl'=2,'y'=4,'rep'=2] {'xl','y'}, dimensions={0} | all-to-all | bytes 1048576 | tf_op jit(solution)/shard_map/all_to_all | solution.py:215
  121.0 4.9 %collective-permute-start.14 = (f32[32,512]{1,0:T(8,128)S(1)}, f32[32,512]{1,0:T(8,128)S(1)}, u32[]{:S(2)}, u32[]{:S(2)}) collective-permute-start(f32[32,512]{1,0:T(8,128)S(1)} %get-tuple-element.35), channel_id=1, source_target_pairs={{0,80},{2,32},{4,0},{6,96},{8,208},{10,160},{12,128},{14,224},{16,... | collective-permute-start | bytes 196616 | tf_op jit(solution)/shard_map/ppermute | solution.py:211
  127.8 5.1 %collective-permute-start.17 = (f32[32,512]{1,0:T(8,128)S(1)}, f32[32,512]{1,0:T(8,128)S(1)}, u32[]{:S(2)}, u32[]{:S(2)}) collective-permute-start(f32[32,512]{1,0:T(8,128)S(1)} %collective-permute-done.14.x_ref), channel_id=1, source_target_pairs={{0,48},{2,50},{4,52},{6,54},{8,56},{10,58},{12,60},{14,62},{16,32}... | collective-permute-start | bytes 196616 | tf_op jit(solution)/shard_map/ppermute | solution.py:211
  135.6 3.0 %collective-permute-done.16.x_ref = f32[32,512]{1,0:T(8,128)S(1)} collective-permute-done((f32[32,512]{1,0:T(8,128)S(1)}, f32[32,512]{1,0:T(8,128)S(1)}, u32[]{:S(2)}, u32[]{:S(2)}) %collective-permute-start.16) | collective-permute-done | bytes 65568 | tf_op jit(solution)/shard_map/ppermute | solution.py:211
  139.5 11.1 %all_to_all.34.parts_ref = f32[8,32,512]{2,1,0:T(8,128)S(1)} all-to-all(f32[8,32,512]{2,1,0:T(8,128)S(1)} %shard_map.50), channel_id=1, replica_groups=mesh['xh'=2,'zh'=4,'zl'=2,'xl'=2,'y'=4,'rep'=2] {'xl','y'}, dimensions={0} | all-to-all | bytes 1048576 | tf_op jit(solution)/shard_map/all_to_all | solution.py:215
  150.7 4.0 %collective-permute-start.18 = (f32[32,512]{1,0:T(8,128)S(1)}, f32[32,512]{1,0:T(8,128)S(1)}, u32[]{:S(2)}, u32[]{:S(2)}) collective-permute-start(f32[32,512]{1,0:T(8,128)S(1)} %get-tuple-element.37), channel_id=1, source_target_pairs={{0,80},{2,32},{4,0},{6,96},{8,208},{10,160},{12,128},{14,224},{16,... | collective-permute-start | bytes 196616 | tf_op jit(solution)/shard_map/ppermute | solution.py:211
  154.7 3.4 %collective-permute-done.18.x_ref = f32[32,512]{1,0:T(8,128)S(1)} collective-permute-done((f32[32,512]{1,0:T(8,128)S(1)}, f32[32,512]{1,0:T(8,128)S(1)}, u32[]{:S(2)}, u32[]{:S(2)}) %collective-permute-start.18) | collective-permute-done | bytes 65568 | tf_op jit(solution)/shard_map/ppermute | solution.py:211
  158.2 3.4 %collective-permute-start.21 = (f32[32,512]{1,0:T(8,128)S(1)}, f32[32,512]{1,0:T(8,128)S(1)}, u32[]{:S(2)}, u32[]{:S(2)}) collective-permute-start(f32[32,512]{1,0:T(8,128)S(1)} %collective-permute-done.18.x_ref), channel_id=1, source_target_pairs={{0,48},{2,50},{4,52},{6,54},{8,56},{10,58},{12,60},{14,62},{16,32}... | collective-permute-start | bytes 196616 | tf_op jit(solution)/shard_map/ppermute | solution.py:211
  167.3 15.4 %all_to_all.35 = f32[8,32,1024]{2,1,0:T(8,128)S(1)} all-to-all(f32[8,32,1024]{2,1,0:T(8,128)S(1)} %shard_map.55), channel_id=1, replica_groups=mesh['xh'=2,'zh'=4,'zl'=2,'xl'=2,'y'=4,'rep'=2] {'xl','y'}, dimensions={0} | all-to-all | bytes 2097152 | tf_op jit(solution)/shard_map/all_to_all | solution.py:215
  (57 shorter events, 31.8 us)
Async XLA Ops:
  0.0 13.1 %copy-start = (f32[32,1024]{1,0:T(8,128)S(1)}, f32[32,1024]{1,0:T(8,128)}, u32[]{:S(2)}) copy-start(f32[32,1024]{1,0:T(8,128)} %vectors_ref.1) | copy-start | bytes 393220
  0.0 12.0 %collective-permute-start = (f32[32,1024]{1,0:T(8,128)}, f32[32,1024]{1,0:T(8,128)S(1)}, u32[]{:S(2)}, u32[]{:S(2)}) collective-permute-start(f32[32,1024]{1,0:T(8,128)} %vectors_ref.1), channel_id=1, source_target_pairs={{0,80},{2,32},{4,0},{6,96},{8,208},{10,160},{12,128},{14,224},{16,... | collective-permute-start | bytes 393224 | tf_op jit(solution)/shard_map/ppermute | solution.py:211
  12.0 5.1 %collective-permute-start.1 = (f32[32,1024]{1,0:T(8,128)S(1)}, f32[32,1024]{1,0:T(8,128)S(1)}, u32[]{:S(2)}, u32[]{:S(2)}) collective-permute-start(f32[32,1024]{1,0:T(8,128)S(1)} %collective-permute-done.x_ref), channel_id=1, source_target_pairs={{0,16},{2,18},{4,20},{6,22},{8,24},{10,26},{12,28},{14,30},{16,0},... | collective-permute-start | bytes 393224 | tf_op jit(solution)/shard_map/ppermute | solution.py:211
  33.3 7.0 %collective-permute-start.2 = (f32[32,512]{1,0:T(8,128)S(1)}, f32[32,512]{1,0:T(8,128)S(1)}, u32[]{:S(2)}, u32[]{:S(2)}) collective-permute-start(f32[32,512]{1,0:T(8,128)S(1)} %get-tuple-element.29), channel_id=1, source_target_pairs={{0,80},{2,32},{4,0},{6,96},{8,208},{10,160},{12,128},{14,224},{16,... | collective-permute-start | bytes 196616 | tf_op jit(solution)/shard_map/ppermute | solution.py:211
  40.2 6.1 %collective-permute-start.5 = (f32[32,512]{1,0:T(8,128)S(1)}, f32[32,512]{1,0:T(8,128)S(1)}, u32[]{:S(2)}, u32[]{:S(2)}) collective-permute-start(f32[32,512]{1,0:T(8,128)S(1)} %collective-permute-done.2.x_ref), channel_id=1, source_target_pairs={{0,48},{2,50},{4,52},{6,54},{8,56},{10,58},{12,60},{14,62},{16,32}... | collective-permute-start | bytes 196616 | tf_op jit(solution)/shard_map/ppermute | solution.py:211
  43.4 4.3 %collective-permute-start.4 = (f32[32,512]{1,0:T(8,128)S(1)}, f32[32,512]{1,0:T(8,128)S(1)}, u32[]{:S(2)}, u32[]{:S(2)}) collective-permute-start(f32[32,512]{1,0:T(8,128)S(1)} %collective-permute-done.2.x_ref), channel_id=1, source_target_pairs={{0,16},{2,18},{4,20},{6,22},{8,24},{10,26},{12,28},{14,30},{16,0},... | collective-permute-start | bytes 196616 | tf_op jit(solution)/shard_map/ppermute | solution.py:211
  43.4 5.2 %collective-permute-start.3 = (f32[32,512]{1,0:T(8,128)S(1)}, f32[32,512]{1,0:T(8,128)S(1)}, u32[]{:S(2)}, u32[]{:S(2)}) collective-permute-start(f32[32,512]{1,0:T(8,128)S(1)} %collective-permute-done.2.x_ref), channel_id=1, source_target_pairs={{0,32},{2,34},{4,36},{6,38},{8,40},{10,42},{12,44},{14,46},{16,48}... | collective-permute-start | bytes 196616 | tf_op jit(solution)/shard_map/ppermute | solution.py:211
  61.8 7.4 %collective-permute-start.6 = (f32[32,512]{1,0:T(8,128)S(1)}, f32[32,512]{1,0:T(8,128)S(1)}, u32[]{:S(2)}, u32[]{:S(2)}) collective-permute-start(f32[32,512]{1,0:T(8,128)S(1)} %get-tuple-element.31), channel_id=1, source_target_pairs={{0,80},{2,32},{4,0},{6,96},{8,208},{10,160},{12,128},{14,224},{16,... | collective-permute-start | bytes 196616 | tf_op jit(solution)/shard_map/ppermute | solution.py:211
  69.3 7.4 %collective-permute-start.9 = (f32[32,512]{1,0:T(8,128)S(1)}, f32[32,512]{1,0:T(8,128)S(1)}, u32[]{:S(2)}, u32[]{:S(2)}) collective-permute-start(f32[32,512]{1,0:T(8,128)S(1)} %collective-permute-done.6.x_ref), channel_id=1, source_target_pairs={{0,48},{2,50},{4,52},{6,54},{8,56},{10,58},{12,60},{14,62},{16,32}... | collective-permute-start | bytes 196616 | tf_op jit(solution)/shard_map/ppermute | solution.py:211
  74.3 4.3 %collective-permute-start.8 = (f32[32,512]{1,0:T(8,128)S(1)}, f32[32,512]{1,0:T(8,128)S(1)}, u32[]{:S(2)}, u32[]{:S(2)}) collective-permute-start(f32[32,512]{1,0:T(8,128)S(1)} %collective-permute-done.6.x_ref), channel_id=1, source_target_pairs={{0,16},{2,18},{4,20},{6,22},{8,24},{10,26},{12,28},{14,30},{16,0},... | collective-permute-start | bytes 196616 | tf_op jit(solution)/shard_map/ppermute | solution.py:211
  74.3 5.2 %collective-permute-start.7 = (f32[32,512]{1,0:T(8,128)S(1)}, f32[32,512]{1,0:T(8,128)S(1)}, u32[]{:S(2)}, u32[]{:S(2)}) collective-permute-start(f32[32,512]{1,0:T(8,128)S(1)} %collective-permute-done.6.x_ref), channel_id=1, source_target_pairs={{0,32},{2,34},{4,36},{6,38},{8,40},{10,42},{12,44},{14,46},{16,48}... | collective-permute-start | bytes 196616 | tf_op jit(solution)/shard_map/ppermute | solution.py:211
  92.3 6.7 %collective-permute-start.10 = (f32[32,512]{1,0:T(8,128)S(1)}, f32[32,512]{1,0:T(8,128)S(1)}, u32[]{:S(2)}, u32[]{:S(2)}) collective-permute-start(f32[32,512]{1,0:T(8,128)S(1)} %get-tuple-element.33), channel_id=1, source_target_pairs={{0,80},{2,32},{4,0},{6,96},{8,208},{10,160},{12,128},{14,224},{16,... | collective-permute-start | bytes 196616 | tf_op jit(solution)/shard_map/ppermute | solution.py:211
  99.1 6.1 %collective-permute-start.13 = (f32[32,512]{1,0:T(8,128)S(1)}, f32[32,512]{1,0:T(8,128)S(1)}, u32[]{:S(2)}, u32[]{:S(2)}) collective-permute-start(f32[32,512]{1,0:T(8,128)S(1)} %collective-permute-done.10.x_ref), channel_id=1, source_target_pairs={{0,48},{2,50},{4,52},{6,54},{8,56},{10,58},{12,60},{14,62},{16,32}... | collective-permute-start | bytes 196616 | tf_op jit(solution)/shard_map/ppermute | solution.py:211
  101.7 4.3 %collective-permute-start.12 = (f32[32,512]{1,0:T(8,128)S(1)}, f32[32,512]{1,0:T(8,128)S(1)}, u32[]{:S(2)}, u32[]{:S(2)}) collective-permute-start(f32[32,512]{1,0:T(8,128)S(1)} %collective-permute-done.10.x_ref), channel_id=1, source_target_pairs={{0,16},{2,18},{4,20},{6,22},{8,24},{10,26},{12,28},{14,30},{16,0},... | collective-permute-start | bytes 196616 | tf_op jit(solution)/shard_map/ppermute | solution.py:211
  101.7 5.2 %collective-permute-start.11 = (f32[32,512]{1,0:T(8,128)S(1)}, f32[32,512]{1,0:T(8,128)S(1)}, u32[]{:S(2)}, u32[]{:S(2)}) collective-permute-start(f32[32,512]{1,0:T(8,128)S(1)} %collective-permute-done.10.x_ref), channel_id=1, source_target_pairs={{0,32},{2,34},{4,36},{6,38},{8,40},{10,42},{12,44},{14,46},{16,48}... | collective-permute-start | bytes 196616 | tf_op jit(solution)/shard_map/ppermute | solution.py:211
  121.0 6.8 %collective-permute-start.14 = (f32[32,512]{1,0:T(8,128)S(1)}, f32[32,512]{1,0:T(8,128)S(1)}, u32[]{:S(2)}, u32[]{:S(2)}) collective-permute-start(f32[32,512]{1,0:T(8,128)S(1)} %get-tuple-element.35), channel_id=1, source_target_pairs={{0,80},{2,32},{4,0},{6,96},{8,208},{10,160},{12,128},{14,224},{16,... | collective-permute-start | bytes 196616 | tf_op jit(solution)/shard_map/ppermute | solution.py:211
  127.8 7.3 %collective-permute-start.17 = (f32[32,512]{1,0:T(8,128)S(1)}, f32[32,512]{1,0:T(8,128)S(1)}, u32[]{:S(2)}, u32[]{:S(2)}) collective-permute-start(f32[32,512]{1,0:T(8,128)S(1)} %collective-permute-done.14.x_ref), channel_id=1, source_target_pairs={{0,48},{2,50},{4,52},{6,54},{8,56},{10,58},{12,60},{14,62},{16,32}... | collective-permute-start | bytes 196616 | tf_op jit(solution)/shard_map/ppermute | solution.py:211
  132.9 5.7 %collective-permute-start.16 = (f32[32,512]{1,0:T(8,128)S(1)}, f32[32,512]{1,0:T(8,128)S(1)}, u32[]{:S(2)}, u32[]{:S(2)}) collective-permute-start(f32[32,512]{1,0:T(8,128)S(1)} %collective-permute-done.14.x_ref), channel_id=1, source_target_pairs={{0,16},{2,18},{4,20},{6,22},{8,24},{10,26},{12,28},{14,30},{16,0},... | collective-permute-start | bytes 196616 | tf_op jit(solution)/shard_map/ppermute | solution.py:211
  132.9 6.1 %collective-permute-start.15 = (f32[32,512]{1,0:T(8,128)S(1)}, f32[32,512]{1,0:T(8,128)S(1)}, u32[]{:S(2)}, u32[]{:S(2)}) collective-permute-start(f32[32,512]{1,0:T(8,128)S(1)} %collective-permute-done.14.x_ref), channel_id=1, source_target_pairs={{0,32},{2,34},{4,36},{6,38},{8,40},{10,42},{12,44},{14,46},{16,48}... | collective-permute-start | bytes 196616 | tf_op jit(solution)/shard_map/ppermute | solution.py:211
  150.7 7.5 %collective-permute-start.18 = (f32[32,512]{1,0:T(8,128)S(1)}, f32[32,512]{1,0:T(8,128)S(1)}, u32[]{:S(2)}, u32[]{:S(2)}) collective-permute-start(f32[32,512]{1,0:T(8,128)S(1)} %get-tuple-element.37), channel_id=1, source_target_pairs={{0,80},{2,32},{4,0},{6,96},{8,208},{10,160},{12,128},{14,224},{16,... | collective-permute-start | bytes 196616 | tf_op jit(solution)/shard_map/ppermute | solution.py:211
  158.2 6.1 %collective-permute-start.21 = (f32[32,512]{1,0:T(8,128)S(1)}, f32[32,512]{1,0:T(8,128)S(1)}, u32[]{:S(2)}, u32[]{:S(2)}) collective-permute-start(f32[32,512]{1,0:T(8,128)S(1)} %collective-permute-done.18.x_ref), channel_id=1, source_target_pairs={{0,48},{2,50},{4,52},{6,54},{8,56},{10,58},{12,60},{14,62},{16,32}... | collective-permute-start | bytes 196616 | tf_op jit(solution)/shard_map/ppermute | solution.py:211
  161.6 4.3 %collective-permute-start.20 = (f32[32,512]{1,0:T(8,128)S(1)}, f32[32,512]{1,0:T(8,128)S(1)}, u32[]{:S(2)}, u32[]{:S(2)}) collective-permute-start(f32[32,512]{1,0:T(8,128)S(1)} %collective-permute-done.18.x_ref), channel_id=1, source_target_pairs={{0,16},{2,18},{4,20},{6,22},{8,24},{10,26},{12,28},{14,30},{16,0},... | collective-permute-start | bytes 196616 | tf_op jit(solution)/shard_map/ppermute | solution.py:211
  161.6 5.2 %collective-permute-start.19 = (f32[32,512]{1,0:T(8,128)S(1)}, f32[32,512]{1,0:T(8,128)S(1)}, u32[]{:S(2)}, u32[]{:S(2)}) collective-permute-start(f32[32,512]{1,0:T(8,128)S(1)} %collective-permute-done.18.x_ref), channel_id=1, source_target_pairs={{0,32},{2,34},{4,36},{6,38},{8,40},{10,42},{12,44},{14,46},{16,48}... | collective-permute-start | bytes 196616 | tf_op jit(solution)/shard_map/ppermute | solution.py:211
where the time goes:
time: 184 us; the launch traced here: 183 us
  blocking collectives  80.6 us (44%)
  starting transfers between devices  55.9 us (30%)
  waiting for transfers between devices  30.6 us (17%)
  Pallas kernels  15.4 us (8%)
    all_to_all x6, blocking collectives, exchange(): return lax.all_to_all(value, COL, 0, 0, tiled=True)  80.6 us
    ppermute x22, starting transfers between devices, permute(): return lax.ppermute(value, ROW + COL, moves)  55.9 us
    ppermute x22, waiting for transfers between devices, permute(): return lax.ppermute(value, ROW + COL, moves)  30.6 us
    pallas_call x27, Pallas kernels, call(): pl.pallas_call(kernel, out_shape=shapes, in_specs=[vmem] * len(operands),...  11.1 us
    pallas_call x1, Pallas kernels, prepare(): pl.pallas_call(prepare_kernel, out_shape=(half, half), in_specs=[pl.Block...  4.29 us
  transfers between devices with their start and end apart: 22, of which 20 were waited for; matrix products, arithmetic and copies ran while one was open for 0% of the time, Pallas kernels for 7%

commit v1 on v0

--- a/solution.py
+++ b/solution.py
@@ -22,7 +22,7 @@
     for y in range(4)
 ]
 FAR = 2
-ARRIVALS = (3, 1, 2)
+ARRIVALS = (1, 3, 2)
 
 
 def index(xh, zh, zl, xl, y):
@@ -162,8 +162,9 @@
         store(start, total, out_ref)
 
 
-def next_kernel(which, x_ref, high_ref, low_ref, before_ref, out_ref):
-    for start, total in tiles([(which, x_ref[...])], high_ref, low_ref, before_ref):
+def two_kernel(x_ref, y_ref, high_ref, low_ref, before_ref, out_ref):
+    pieces = [(which, ref[...]) for which, ref in zip(ARRIVALS, (x_ref, y_ref))]
+    for start, total in tiles(pieces, high_ref, low_ref, before_ref):
         store(start, total, out_ref)
 
 
@@ -233,9 +234,8 @@
     for which in ARRIVALS:
         others[which] = permute(piece, partner_moves(which))
     total = call(own_kernel, (vectors, rows), FLOPS, LIMIT, piece, *halves)
-    for which in ARRIVALS[:2]:
-        kernel = functools.partial(next_kernel, which)
-        total = call(kernel, (vectors, rows), FLOPS, LIMIT, others[which], *halves, total)
+    arrived = [others[which] for which in ARRIVALS[:2]]
+    total = call(two_kernel, (vectors, rows), 2 * FLOPS, LIMIT, *arrived, *halves, total)
     which = ARRIVALS[2]
     if running is None:
         kernel = functools.partial(spread_kernel, which)

time: 184 us -> 184 us (level)
    pallas_call x27 -> x22, Pallas kernels: 11.1 us -> 10.6 us  [call(): pl.pallas_call(kernel, out_shape=shapes, in_specs=[vmem] * len(operands),...]
  transfers between devices with their start and end apart: 22 -> 22, of which waited for: 20 -> 19; matrix products, arithmetic and copies ran while one was open for 0% -> 0% of each run, Pallas kernels for 7% -> 6%
where the time goes in v1:
time: 184 us; the launch traced here: 183 us
  blocking collectives  79.7 us (43%)
  starting transfers between devices  55.6 us (30%)
  waiting for transfers between devices  32.1 us (17%)
  Pallas kernels  14.9 us (8%)
    all_to_all x6, blocking collectives, exchange(): return lax.all_to_all(value, COL, 0, 0, tiled=True)  79.7 us
    ppermute x22, starting transfers between devices, permute(): return lax.ppermute(value, ROW + COL, moves)  55.6 us
    ppermute x22, waiting for transfers between devices, permute(): return lax.ppermute(value, ROW + COL, moves)  32.1 us
    pallas_call x22, Pallas kernels, call(): pl.pallas_call(kernel, out_shape=shapes, in_specs=[vmem] * len(operands),...  10.6 us
    pallas_call x1, Pallas kernels, prepare(): pl.pallas_call(prepare_kernel, out_shape=(half, half), in_specs=[pl.Block...  4.29 us
  transfers between devices with their start and end apart: 22, of which 19 were waited for; matrix products, arithmetic and copies ran while one was open for 0% of the time, Pallas kernels for 6%

profile of v1, /device:TPU:2, one launch (start us, length us, event | category | flops | bytes accessed | tf_op | source)
XLA Modules:
  0.0 183.1 jit_solution(8723505053057139878)
XLA Ops:
  0.0 7.7 %collective-permute-start = (f32[32,1024]{1,0:T(8,128)}, f32[32,1024]{1,0:T(8,128)S(1)}, u32[]{:S(2)}, u32[]{:S(2)}) collective-permute-start(f32[32,1024]{1,0:T(8,128)} %vectors_ref.1), channel_id=1, source_target_pairs={{0,80},{2,32},{4,0},{6,96},{8,208},{10,160},{12,128},{14,224},{16,... | collective-permute-start | bytes 393224 | tf_op jit(solution)/shard_map/ppermute | solution.py:212
  7.7 4.3 %shard_map.28 = (bf16[2048,1024]{1,0:T(8,128)(2,1)S(1)}, bf16[2048,1024]{1,0:T(8,128)(2,1)S(1)}) custom-call(f32[1024,2048]{1,0:T(8,128)} %a_ref.1), custom_call_target="tpu_custom_call" | custom-call | flops 4000000000 | bytes 8388608 | tf_op jit(solution)/shard_map/pallas_call | solution.py:93
  13.9 3.1 %collective-permute-done.1.x_ref = f32[32,1024]{1,0:T(8,128)S(1)} collective-permute-done((f32[32,1024]{1,0:T(8,128)S(1)}, f32[32,1024]{1,0:T(8,128)S(1)}, u32[]{:S(2)}, u32[]{:S(2)}) %collective-permute-start.1) | collective-permute-done | bytes 131104 | tf_op jit(solution)/shard_map/ppermute | solution.py:212
  17.9 15.4 %all_to_all.30.parts_ref = f32[8,32,512]{2,1,0:T(8,128)S(1)} all-to-all(f32[8,32,512]{2,1,0:T(8,128)S(1)} %shard_map.30), channel_id=1, replica_groups=mesh['xh'=2,'zh'=4,'zl'=2,'xl'=2,'y'=4,'rep'=2] {'xl','y'}, dimensions={0} | all-to-all | bytes 1048576 | tf_op jit(solution)/shard_map/all_to_all | solution.py:216
  33.3 4.0 %collective-permute-start.2 = (f32[32,512]{1,0:T(8,128)S(1)}, f32[32,512]{1,0:T(8,128)S(1)}, u32[]{:S(2)}, u32[]{:S(2)}) collective-permute-start(f32[32,512]{1,0:T(8,128)S(1)} %get-tuple-element.29), channel_id=1, source_target_pairs={{0,80},{2,32},{4,0},{6,96},{8,208},{10,160},{12,128},{14,224},{16,... | collective-permute-start | bytes 196616 | tf_op jit(solution)/shard_map/ppermute | solution.py:212
  37.3 2.9 %collective-permute-done.2.x_ref = f32[32,512]{1,0:T(8,128)S(1)} collective-permute-done((f32[32,512]{1,0:T(8,128)S(1)}, f32[32,512]{1,0:T(8,128)S(1)}, u32[]{:S(2)}, u32[]{:S(2)}) %collective-permute-start.2) | collective-permute-done | bytes 65568 | tf_op jit(solution)/shard_map/ppermute | solution.py:212
  40.2 3.2 %collective-permute-start.5 = (f32[32,512]{1,0:T(8,128)S(1)}, f32[32,512]{1,0:T(8,128)S(1)}, u32[]{:S(2)}, u32[]{:S(2)}) collective-permute-start(f32[32,512]{1,0:T(8,128)S(1)} %collective-permute-done.2.x_ref), channel_id=1, source_target_pairs={{0,48},{2,50},{4,52},{6,54},{8,56},{10,58},{12,60},{14,62},{16,32}... | collective-permute-start | bytes 196616 | tf_op jit(solution)/shard_map/ppermute | solution.py:212
  49.1 12.8 %all_to_all.31.parts_ref = f32[8,32,512]{2,1,0:T(8,128)S(1)} all-to-all(f32[8,32,512]{2,1,0:T(8,128)S(1)} %shard_map.34), channel_id=1, replica_groups=mesh['xh'=2,'zh'=4,'zl'=2,'xl'=2,'y'=4,'rep'=2] {'xl','y'}, dimensions={0} | all-to-all | bytes 1048576 | tf_op jit(solution)/shard_map/all_to_all | solution.py:216
  61.8 5.5 %collective-permute-start.6 = (f32[32,512]{1,0:T(8,128)S(1)}, f32[32,512]{1,0:T(8,128)S(1)}, u32[]{:S(2)}, u32[]{:S(2)}) collective-permute-start(f32[32,512]{1,0:T(8,128)S(1)} %get-tuple-element.31), channel_id=1, source_target_pairs={{0,80},{2,32},{4,0},{6,96},{8,208},{10,160},{12,128},{14,224},{16,... | collective-permute-start | bytes 196616 | tf_op jit(solution)/shard_map/ppermute | solution.py:212
  69.3 5.0 %collective-permute-start.9 = (f32[32,512]{1,0:T(8,128)S(1)}, f32[32,512]{1,0:T(8,128)S(1)}, u32[]{:S(2)}, u32[]{:S(2)}) collective-permute-start(f32[32,512]{1,0:T(8,128)S(1)} %collective-permute-done.6.x_ref), channel_id=1, source_target_pairs={{0,48},{2,50},{4,52},{6,54},{8,56},{10,58},{12,60},{14,62},{16,32}... | collective-permute-start | bytes 196616 | tf_op jit(solution)/shard_map/ppermute | solution.py:212
  80.0 12.6 %all_to_all.32.parts_ref = f32[8,32,512]{2,1,0:T(8,128)S(1)} all-to-all(f32[8,32,512]{2,1,0:T(8,128)S(1)} %shard_map.38), channel_id=1, replica_groups=mesh['xh'=2,'zh'=4,'zl'=2,'xl'=2,'y'=4,'rep'=2] {'xl','y'}, dimensions={0} | all-to-all | bytes 1048576 | tf_op jit(solution)/shard_map/all_to_all | solution.py:216
  92.6 4.0 %collective-permute-start.10 = (f32[32,512]{1,0:T(8,128)S(1)}, f32[32,512]{1,0:T(8,128)S(1)}, u32[]{:S(2)}, u32[]{:S(2)}) collective-permute-start(f32[32,512]{1,0:T(8,128)S(1)} %get-tuple-element.33), channel_id=1, source_target_pairs={{0,80},{2,32},{4,0},{6,96},{8,208},{10,160},{12,128},{14,224},{16,... | collective-permute-start | bytes 196616 | tf_op jit(solution)/shard_map/ppermute | solution.py:212
  96.6 2.8 %collective-permute-done.10.x_ref = f32[32,512]{1,0:T(8,128)S(1)} collective-permute-done((f32[32,512]{1,0:T(8,128)S(1)}, f32[32,512]{1,0:T(8,128)S(1)}, u32[]{:S(2)}, u32[]{:S(2)}) %collective-permute-start.10) | collective-permute-done | bytes 65568 | tf_op jit(solution)/shard_map/ppermute | solution.py:212
  99.3 2.1 %collective-permute-start.13 = (f32[32,512]{1,0:T(8,128)S(1)}, f32[32,512]{1,0:T(8,128)S(1)}, u32[]{:S(2)}, u32[]{:S(2)}) collective-permute-start(f32[32,512]{1,0:T(8,128)S(1)} %collective-permute-done.10.x_ref), channel_id=1, source_target_pairs={{0,48},{2,50},{4,52},{6,54},{8,56},{10,58},{12,60},{14,62},{16,32}... | collective-permute-start | bytes 196616 | tf_op jit(solution)/shard_map/ppermute | solution.py:212
  101.4 2.3 %collective-permute-start.11 = (f32[32,512]{1,0:T(8,128)S(1)}, f32[32,512]{1,0:T(8,128)S(1)}, u32[]{:S(2)}, u32[]{:S(2)}) collective-permute-start(f32[32,512]{1,0:T(8,128)S(1)} %collective-permute-done.10.x_ref), channel_id=1, source_target_pairs={{0,32},{2,34},{4,36},{6,38},{8,40},{10,42},{12,44},{14,46},{16,48}... | collective-permute-start | bytes 196616 | tf_op jit(solution)/shard_map/ppermute | solution.py:212
  108.1 12.8 %all_to_all.33.parts_ref = f32[8,32,512]{2,1,0:T(8,128)S(1)} all-to-all(f32[8,32,512]{2,1,0:T(8,128)S(1)} %shard_map.42), channel_id=1, replica_groups=mesh['xh'=2,'zh'=4,'zl'=2,'xl'=2,'y'=4,'rep'=2] {'xl','y'}, dimensions={0} | all-to-all | bytes 1048576 | tf_op jit(solution)/shard_map/all_to_all | solution.py:216
  121.0 5.0 %collective-permute-start.14 = (f32[32,512]{1,0:T(8,128)S(1)}, f32[32,512]{1,0:T(8,128)S(1)}, u32[]{:S(2)}, u32[]{:S(2)}) collective-permute-start(f32[32,512]{1,0:T(8,128)S(1)} %get-tuple-element.35), channel_id=1, source_target_pairs={{0,80},{2,32},{4,0},{6,96},{8,208},{10,160},{12,128},{14,224},{16,... | collective-permute-start | bytes 196616 | tf_op jit(solution)/shard_map/ppermute | solution.py:212
  127.8 5.1 %collective-permute-start.17 = (f32[32,512]{1,0:T(8,128)S(1)}, f32[32,512]{1,0:T(8,128)S(1)}, u32[]{:S(2)}, u32[]{:S(2)}) collective-permute-start(f32[32,512]{1,0:T(8,128)S(1)} %collective-permute-done.14.x_ref), channel_id=1, source_target_pairs={{0,48},{2,50},{4,52},{6,54},{8,56},{10,58},{12,60},{14,62},{16,32}... | collective-permute-start | bytes 196616 | tf_op jit(solution)/shard_map/ppermute | solution.py:212
  135.2 3.4 %collective-permute-done.16.x_ref = f32[32,512]{1,0:T(8,128)S(1)} collective-permute-done((f32[32,512]{1,0:T(8,128)S(1)}, f32[32,512]{1,0:T(8,128)S(1)}, u32[]{:S(2)}, u32[]{:S(2)}) %collective-permute-start.16) | collective-permute-done | bytes 65568 | tf_op jit(solution)/shard_map/ppermute | solution.py:212
  139.9 10.9 %all_to_all.34.parts_ref = f32[8,32,512]{2,1,0:T(8,128)S(1)} all-to-all(f32[8,32,512]{2,1,0:T(8,128)S(1)} %shard_map.46), channel_id=1, replica_groups=mesh['xh'=2,'zh'=4,'zl'=2,'xl'=2,'y'=4,'rep'=2] {'xl','y'}, dimensions={0} | all-to-all | bytes 1048576 | tf_op jit(solution)/shard_map/all_to_all | solution.py:216
  150.8 3.9 %collective-permute-start.18 = (f32[32,512]{1,0:T(8,128)S(1)}, f32[32,512]{1,0:T(8,128)S(1)}, u32[]{:S(2)}, u32[]{:S(2)}) collective-permute-start(f32[32,512]{1,0:T(8,128)S(1)} %get-tuple-element.37), channel_id=1, source_target_pairs={{0,80},{2,32},{4,0},{6,96},{8,208},{10,160},{12,128},{14,224},{16,... | collective-permute-start | bytes 196616 | tf_op jit(solution)/shard_map/ppermute | solution.py:212
  154.7 3.8 %collective-permute-done.18.x_ref = f32[32,512]{1,0:T(8,128)S(1)} collective-permute-done((f32[32,512]{1,0:T(8,128)S(1)}, f32[32,512]{1,0:T(8,128)S(1)}, u32[]{:S(2)}, u32[]{:S(2)}) %collective-permute-start.18) | collective-permute-done | bytes 65568 | tf_op jit(solution)/shard_map/ppermute | solution.py:212
  158.5 2.9 %collective-permute-start.21 = (f32[32,512]{1,0:T(8,128)S(1)}, f32[32,512]{1,0:T(8,128)S(1)}, u32[]{:S(2)}, u32[]{:S(2)}) collective-permute-start(f32[32,512]{1,0:T(8,128)S(1)} %collective-permute-done.18.x_ref), channel_id=1, source_target_pairs={{0,48},{2,50},{4,52},{6,54},{8,56},{10,58},{12,60},{14,62},{16,32}... | collective-permute-start | bytes 196616 | tf_op jit(solution)/shard_map/ppermute | solution.py:212
  167.0 15.3 %all_to_all.35 = f32[8,32,1024]{2,1,0:T(8,128)S(1)} all-to-all(f32[8,32,1024]{2,1,0:T(8,128)S(1)} %shard_map.50), channel_id=1, replica_groups=mesh['xh'=2,'zh'=4,'zl'=2,'xl'=2,'y'=4,'rep'=2] {'xl','y'}, dimensions={0} | all-to-all | bytes 2097152 | tf_op jit(solution)/shard_map/all_to_all | solution.py:216
  (52 shorter events, 32.3 us)
Async XLA Ops:
  0.0 13.1 %copy-start = (f32[32,1024]{1,0:T(8,128)S(1)}, f32[32,1024]{1,0:T(8,128)}, u32[]{:S(2)}) copy-start(f32[32,1024]{1,0:T(8,128)} %vectors_ref.1) | copy-start | bytes 393220
  0.0 12.0 %collective-permute-start = (f32[32,1024]{1,0:T(8,128)}, f32[32,1024]{1,0:T(8,128)S(1)}, u32[]{:S(2)}, u32[]{:S(2)}) collective-permute-start(f32[32,1024]{1,0:T(8,128)} %vectors_ref.1), channel_id=1, source_target_pairs={{0,80},{2,32},{4,0},{6,96},{8,208},{10,160},{12,128},{14,224},{16,... | collective-permute-start | bytes 393224 | tf_op jit(solution)/shard_map/ppermute | solution.py:212
  12.0 5.1 %collective-permute-start.1 = (f32[32,1024]{1,0:T(8,128)S(1)}, f32[32,1024]{1,0:T(8,128)S(1)}, u32[]{:S(2)}, u32[]{:S(2)}) collective-permute-start(f32[32,1024]{1,0:T(8,128)S(1)} %collective-permute-done.x_ref), channel_id=1, source_target_pairs={{0,16},{2,18},{4,20},{6,22},{8,24},{10,26},{12,28},{14,30},{16,0},... | collective-permute-start | bytes 393224 | tf_op jit(solution)/shard_map/ppermute | solution.py:212
  33.3 7.0 %collective-permute-start.2 = (f32[32,512]{1,0:T(8,128)S(1)}, f32[32,512]{1,0:T(8,128)S(1)}, u32[]{:S(2)}, u32[]{:S(2)}) collective-permute-start(f32[32,512]{1,0:T(8,128)S(1)} %get-tuple-element.29), channel_id=1, source_target_pairs={{0,80},{2,32},{4,0},{6,96},{8,208},{10,160},{12,128},{14,224},{16,... | collective-permute-start | bytes 196616 | tf_op jit(solution)/shard_map/ppermute | solution.py:212
  40.2 6.1 %collective-permute-start.5 = (f32[32,512]{1,0:T(8,128)S(1)}, f32[32,512]{1,0:T(8,128)S(1)}, u32[]{:S(2)}, u32[]{:S(2)}) collective-permute-start(f32[32,512]{1,0:T(8,128)S(1)} %collective-permute-done.2.x_ref), channel_id=1, source_target_pairs={{0,48},{2,50},{4,52},{6,54},{8,56},{10,58},{12,60},{14,62},{16,32}... | collective-permute-start | bytes 196616 | tf_op jit(solution)/shard_map/ppermute | solution.py:212
  43.4 4.3 %collective-permute-start.4 = (f32[32,512]{1,0:T(8,128)S(1)}, f32[32,512]{1,0:T(8,128)S(1)}, u32[]{:S(2)}, u32[]{:S(2)}) collective-permute-start(f32[32,512]{1,0:T(8,128)S(1)} %collective-permute-done.2.x_ref), channel_id=1, source_target_pairs={{0,16},{2,18},{4,20},{6,22},{8,24},{10,26},{12,28},{14,30},{16,0},... | collective-permute-start | bytes 196616 | tf_op jit(solution)/shard_map/ppermute | solution.py:212
  43.4 5.2 %collective-permute-start.3 = (f32[32,512]{1,0:T(8,128)S(1)}, f32[32,512]{1,0:T(8,128)S(1)}, u32[]{:S(2)}, u32[]{:S(2)}) collective-permute-start(f32[32,512]{1,0:T(8,128)S(1)} %collective-permute-done.2.x_ref), channel_id=1, source_target_pairs={{0,32},{2,34},{4,36},{6,38},{8,40},{10,42},{12,44},{14,46},{16,48}... | collective-permute-start | bytes 196616 | tf_op jit(solution)/shard_map/ppermute | solution.py:212
  61.8 7.4 %collective-permute-start.6 = (f32[32,512]{1,0:T(8,128)S(1)}, f32[32,512]{1,0:T(8,128)S(1)}, u32[]{:S(2)}, u32[]{:S(2)}) collective-permute-start(f32[32,512]{1,0:T(8,128)S(1)} %get-tuple-element.31), channel_id=1, source_target_pairs={{0,80},{2,32},{4,0},{6,96},{8,208},{10,160},{12,128},{14,224},{16,... | collective-permute-start | bytes 196616 | tf_op jit(solution)/shard_map/ppermute | solution.py:212
  69.3 7.4 %collective-permute-start.9 = (f32[32,512]{1,0:T(8,128)S(1)}, f32[32,512]{1,0:T(8,128)S(1)}, u32[]{:S(2)}, u32[]{:S(2)}) collective-permute-start(f32[32,512]{1,0:T(8,128)S(1)} %collective-permute-done.6.x_ref), channel_id=1, source_target_pairs={{0,48},{2,50},{4,52},{6,54},{8,56},{10,58},{12,60},{14,62},{16,32}... | collective-permute-start | bytes 196616 | tf_op jit(solution)/shard_map/ppermute | solution.py:212
  74.3 4.3 %collective-permute-start.8 = (f32[32,512]{1,0:T(8,128)S(1)}, f32[32,512]{1,0:T(8,128)S(1)}, u32[]{:S(2)}, u32[]{:S(2)}) collective-permute-start(f32[32,512]{1,0:T(8,128)S(1)} %collective-permute-done.6.x_ref), channel_id=1, source_target_pairs={{0,16},{2,18},{4,20},{6,22},{8,24},{10,26},{12,28},{14,30},{16,0},... | collective-permute-start | bytes 196616 | tf_op jit(solution)/shard_map/ppermute | solution.py:212
  74.3 5.2 %collective-permute-start.7 = (f32[32,512]{1,0:T(8,128)S(1)}, f32[32,512]{1,0:T(8,128)S(1)}, u32[]{:S(2)}, u32[]{:S(2)}) collective-permute-start(f32[32,512]{1,0:T(8,128)S(1)} %collective-permute-done.6.x_ref), channel_id=1, source_target_pairs={{0,32},{2,34},{4,36},{6,38},{8,40},{10,42},{12,44},{14,46},{16,48}... | collective-permute-start | bytes 196616 | tf_op jit(solution)/shard_map/ppermute | solution.py:212
  92.6 6.7 %collective-permute-start.10 = (f32[32,512]{1,0:T(8,128)S(1)}, f32[32,512]{1,0:T(8,128)S(1)}, u32[]{:S(2)}, u32[]{:S(2)}) collective-permute-start(f32[32,512]{1,0:T(8,128)S(1)} %get-tuple-element.33), channel_id=1, source_target_pairs={{0,80},{2,32},{4,0},{6,96},{8,208},{10,160},{12,128},{14,224},{16,... | collective-permute-start | bytes 196616 | tf_op jit(solution)/shard_map/ppermute | solution.py:212
  99.3 6.1 %collective-permute-start.13 = (f32[32,512]{1,0:T(8,128)S(1)}, f32[32,512]{1,0:T(8,128)S(1)}, u32[]{:S(2)}, u32[]{:S(2)}) collective-permute-start(f32[32,512]{1,0:T(8,128)S(1)} %collective-permute-done.10.x_ref), channel_id=1, source_target_pairs={{0,48},{2,50},{4,52},{6,54},{8,56},{10,58},{12,60},{14,62},{16,32}... | collective-permute-start | bytes 196616 | tf_op jit(solution)/shard_map/ppermute | solution.py:212
  101.4 5.4 %collective-permute-start.12 = (f32[32,512]{1,0:T(8,128)S(1)}, f32[32,512]{1,0:T(8,128)S(1)}, u32[]{:S(2)}, u32[]{:S(2)}) collective-permute-start(f32[32,512]{1,0:T(8,128)S(1)} %collective-permute-done.10.x_ref), channel_id=1, source_target_pairs={{0,16},{2,18},{4,20},{6,22},{8,24},{10,26},{12,28},{14,30},{16,0},... | collective-permute-start | bytes 196616 | tf_op jit(solution)/shard_map/ppermute | solution.py:212
  101.4 6.2 %collective-permute-start.11 = (f32[32,512]{1,0:T(8,128)S(1)}, f32[32,512]{1,0:T(8,128)S(1)}, u32[]{:S(2)}, u32[]{:S(2)}) collective-permute-start(f32[32,512]{1,0:T(8,128)S(1)} %collective-permute-done.10.x_ref), channel_id=1, source_target_pairs={{0,32},{2,34},{4,36},{6,38},{8,40},{10,42},{12,44},{14,46},{16,48}... | collective-permute-start | bytes 196616 | tf_op jit(solution)/shard_map/ppermute | solution.py:212
  121.0 6.9 %collective-permute-start.14 = (f32[32,512]{1,0:T(8,128)S(1)}, f32[32,512]{1,0:T(8,128)S(1)}, u32[]{:S(2)}, u32[]{:S(2)}) collective-permute-start(f32[32,512]{1,0:T(8,128)S(1)} %get-tuple-element.35), channel_id=1, source_target_pairs={{0,80},{2,32},{4,0},{6,96},{8,208},{10,160},{12,128},{14,224},{16,... | collective-permute-start | bytes 196616 | tf_op jit(solution)/shard_map/ppermute | solution.py:212
  127.8 7.4 %collective-permute-start.17 = (f32[32,512]{1,0:T(8,128)S(1)}, f32[32,512]{1,0:T(8,128)S(1)}, u32[]{:S(2)}, u32[]{:S(2)}) collective-permute-start(f32[32,512]{1,0:T(8,128)S(1)} %collective-permute-done.14.x_ref), channel_id=1, source_target_pairs={{0,48},{2,50},{4,52},{6,54},{8,56},{10,58},{12,60},{14,62},{16,32}... | collective-permute-start | bytes 196616 | tf_op jit(solution)/shard_map/ppermute | solution.py:212
  132.9 5.7 %collective-permute-start.16 = (f32[32,512]{1,0:T(8,128)S(1)}, f32[32,512]{1,0:T(8,128)S(1)}, u32[]{:S(2)}, u32[]{:S(2)}) collective-permute-start(f32[32,512]{1,0:T(8,128)S(1)} %collective-permute-done.14.x_ref), channel_id=1, source_target_pairs={{0,16},{2,18},{4,20},{6,22},{8,24},{10,26},{12,28},{14,30},{16,0},... | collective-permute-start | bytes 196616 | tf_op jit(solution)/shard_map/ppermute | solution.py:212
  132.9 6.5 %collective-permute-start.15 = (f32[32,512]{1,0:T(8,128)S(1)}, f32[32,512]{1,0:T(8,128)S(1)}, u32[]{:S(2)}, u32[]{:S(2)}) collective-permute-start(f32[32,512]{1,0:T(8,128)S(1)} %collective-permute-done.14.x_ref), channel_id=1, source_target_pairs={{0,32},{2,34},{4,36},{6,38},{8,40},{10,42},{12,44},{14,46},{16,48}... | collective-permute-start | bytes 196616 | tf_op jit(solution)/shard_map/ppermute | solution.py:212
  150.8 7.6 %collective-permute-start.18 = (f32[32,512]{1,0:T(8,128)S(1)}, f32[32,512]{1,0:T(8,128)S(1)}, u32[]{:S(2)}, u32[]{:S(2)}) collective-permute-start(f32[32,512]{1,0:T(8,128)S(1)} %get-tuple-element.37), channel_id=1, source_target_pairs={{0,80},{2,32},{4,0},{6,96},{8,208},{10,160},{12,128},{14,224},{16,... | collective-permute-start | bytes 196616 | tf_op jit(solution)/shard_map/ppermute | solution.py:212
  158.5 6.1 %collective-permute-start.21 = (f32[32,512]{1,0:T(8,128)S(1)}, f32[32,512]{1,0:T(8,128)S(1)}, u32[]{:S(2)}, u32[]{:S(2)}) collective-permute-start(f32[32,512]{1,0:T(8,128)S(1)} %collective-permute-done.18.x_ref), channel_id=1, source_target_pairs={{0,48},{2,50},{4,52},{6,54},{8,56},{10,58},{12,60},{14,62},{16,32}... | collective-permute-start | bytes 196616 | tf_op jit(solution)/shard_map/ppermute | solution.py:212
  161.4 4.3 %collective-permute-start.20 = (f32[32,512]{1,0:T(8,128)S(1)}, f32[32,512]{1,0:T(8,128)S(1)}, u32[]{:S(2)}, u32[]{:S(2)}) collective-permute-start(f32[32,512]{1,0:T(8,128)S(1)} %collective-permute-done.18.x_ref), channel_id=1, source_target_pairs={{0,16},{2,18},{4,20},{6,22},{8,24},{10,26},{12,28},{14,30},{16,0},... | collective-permute-start | bytes 196616 | tf_op jit(solution)/shard_map/ppermute | solution.py:212
  161.4 5.2 %collective-permute-start.19 = (f32[32,512]{1,0:T(8,128)S(1)}, f32[32,512]{1,0:T(8,128)S(1)}, u32[]{:S(2)}, u32[]{:S(2)}) collective-permute-start(f32[32,512]{1,0:T(8,128)S(1)} %collective-permute-done.18.x_ref), channel_id=1, source_target_pairs={{0,32},{2,34},{4,36},{6,38},{8,40},{10,42},{12,44},{14,46},{16,48}... | collective-permute-start | bytes 196616 | tf_op jit(solution)/shard_map/ppermute | solution.py:212
